TPU v7x, 32 devices: a whole 2x2x4 slice. The times are simulated.
32 devices in a mesh: gx: 2 (over y), gy: 4 (over x, core), gz: 4 (over z).
Axes of the slice: x: 2, y: 2, z: 4, core: 2. Of those that a mesh axis runs over, the one named last changes fastest.
Arguments:
- log_range: float32 [64, 128, 512], P('gx', 'gy', 'gz'), may hold values from 0.7 to 2
- state: float32 [2, 64, 128, 512], P(None, 'gx', 'gy', 'gz'), may hold values from -60 to 60, as said below
- adjoint_start: float32 [2, 64, 128, 512], P(None, 'gx', 'gy', 'gz'), may hold values from -0.3 to 0.3
- obs_index: int32 [2, 2, 4, 4, 4096], P(None, 'gx', 'gy', 'gz'), may hold values from 0 to 131071
- obs_value: float32 [2, 2, 4, 4, 4096], P(None, 'gx', 'gy', 'gz'), may hold values from -6 to 6
Outputs:
- gradient: float32 [64, 128, 512], P('gx', 'gy', 'gz')
- adjoint: float32 [2, 64, 128, 512], P(None, 'gx', 'gy', 'gz')
Inputs may be any that keep to these rules, and one draw needn't show every extreme that they name: `obs_index`: each entry numbers a cell of its own device's block as (a * 32 + b) * 128 + c; cells may repeat. `state`: real values.
All inputs are finite; a program needn't handle non-finite values.
Results may differ from a plain program's by a relative error of at most 0.0001.
Values sent between devices are 32-bit elements; how exact they have to be, the bound alone decides.
A program may use at most 320 MiB of HBM per device.

v0:
```python
import jax
import jax.numpy as jnp
from jax import lax
from jax.sharding import PartitionSpec as P

ITERS = 4


noise_var = 0.25


def with_halo(shard, sides, width):
    for axis, dim in sides:
        peers, length = (lax.axis_size(axis), shard.shape[dim])
        up = [(i, (i + 1) % peers) for i in range(peers)]
        down = [(j, i) for i, j in up]
        last = lax.slice_in_dim(shard, length - width, length, axis=dim)
        leading = lax.slice_in_dim(shard, 0, width, axis=dim)
        before = lax.ppermute(last, axis, up)
        after = lax.ppermute(leading, axis, down)
        shard = jnp.concatenate([before, shard, after], axis=dim)
    return shard


def stencil(padded, center, kappa_sq):
    beside = padded[:, 2:, 1:-1, 1:-1] + padded[:, :-2, 1:-1, 1:-1]
    beside = beside + padded[:, 1:-1, 2:, 1:-1] + padded[:, 1:-1, :-2, 1:-1]
    beside = beside + padded[:, 1:-1, 1:-1, 2:] + padded[:, 1:-1, 1:-1, :-2]
    return (kappa_sq[None] + 6.0) * center - beside


def one_pass(field, kappa_sq):
    padded = with_halo(field, (("gx", 1), ("gy", 2), ("gz", 3)), 1)
    return stencil(padded, field, kappa_sq)


def two_products(residual, image):
    return lax.psum(
        (jnp.sum(residual * residual, axis=(1, 2, 3)), jnp.sum(residual * image, axis=(1, 2, 3))),
        ("gx", "gy", "gz"),
    )


def widen(values):
    return values[:, None, None, None]


def on_device(log_range, state, adjoint_start, obs_index, obs_value):
    replicas = state.shape[0]
    field_shape = state.shape
    cells = field_shape[1] * field_shape[2] * field_shape[3]
    kappa_sq = 4.0 * jnp.exp(-2.0 * log_range)
    observed = obs_index.reshape(replicas, -1)
    measured = obs_value.reshape(replicas, -1)
    row_ids = jnp.arange(replicas, dtype=jnp.int32)[:, None]
    payload = jnp.stack([jnp.ones_like(measured), measured], 0)
    scattered = jnp.zeros((2, replicas, cells), jnp.float32).at[:, row_ids, observed].add(payload)
    counted = scattered[0].reshape(field_shape)
    value_sum = scattered[1].reshape(field_shape)
    obs_weight = counted / noise_var
    right_side = (value_sum - counted * state) / noise_var

    def first_image(stack):
        applied = one_pass(stack, kappa_sq)
        return (applied, applied)

    def second_image(inner):
        return one_pass(inner, kappa_sq)

    def system(vector):
        inner, applied = first_image(vector)
        return (second_image(inner) + obs_weight * vector, applied)

    adjoint = adjoint_start
    start_image, unused = system(adjoint)
    residual = right_side - start_image
    image, residual_image = system(residual)
    norm_now, product = two_products(residual, image)
    step_size = norm_now / product
    direction, along = (residual, image)
    direction_image = residual_image
    for iteration in range(ITERS):
        adjoint = adjoint + widen(step_size) * direction
        if iteration + 1 < ITERS:
            residual = residual - widen(step_size) * along
            image, residual_image = system(residual)
            norm_next, product = two_products(residual, image)
            ratio = norm_next / norm_now
            step_size = norm_next / (product - ratio * norm_next / step_size)
            direction = residual + widen(ratio) * direction
            direction_image = residual_image + widen(ratio) * direction_image
            along = image + widen(ratio) * along
            norm_now = norm_next
    joined = jnp.concatenate([state, adjoint], 0)
    padded = with_halo(joined, (("gx", 1), ("gy", 2), ("gz", 3)), 1)
    images = stencil(padded, joined, kappa_sq)
    state_image = images[:replicas]
    adjoint_image = images[replicas:]
    terms = -2.0 * kappa_sq[None] * (adjoint * state_image + adjoint_image * state)
    gradient = jnp.sum(terms, axis=0)
    return (gradient, adjoint)


def solution(mesh):
    in_specs = (
        P("gx", "gy", "gz"),
        P(None, "gx", "gy", "gz"),
        P(None, "gx", "gy", "gz"),
        P(None, "gx", "gy", "gz", None),
        P(None, "gx", "gy", "gz", None),
    )
    out_specs = (P("gx", "gy", "gz"), P(None, "gx", "gy", "gz"))
    return jax.shard_map(
        on_device, mesh=mesh, in_specs=in_specs, out_specs=out_specs, check_vma=False
    )
```

profile of v0, /device:TPU:0, one launch (start us, length us, event | category | flops | bytes accessed | tf_op | source)
XLA Modules:
  0.0 776.4 jit_solution(16770681192039878045)
XLA Ops:
  1.5 3.0 collective-permute-start
  5.4 2.0 fusion.84
  17.9 2.2 collective-permute-start.4
  25.7 4.4 fusion.79
  32.3 5.9 sort
  40.4 2.7 copy.8
  43.0 149.9 %scatter_custom_fusion = f32[2,262144]{0,1:T(8,128)} fusion(s32[8192]{0:T(1024)S(1)} %get-tuple-element.2, f32[]{:T(128)} %constant.10.clone.1, f32[8192,2]{1,0:T(8,128)} %copy.8, s32[8192]{0:T(1024)S(1)} %broadcast_clamp_fusion), kind=kCustom, calls=%fused_computation.4 | custom fusion | flops 16384 | bytes 2097664
  199.0 2.1 collective-permute-start.10
  201.1 131.2 %slice_reduce_fusion = (f32[262144]{0:T(1024)S(1)}, f32[262144]{0:T(1024)}) fusion(f32[2,262144]{0,1:T(8,128)} %scatter_custom_fusion), kind=kLoop, calls=%fused_computation.2 | loop fusion | bytes 4194304 | tf_op jit(solution)/shard_map/slice | solution.py:58
  335.7 6.4 fusion.73
  347.2 2.1 collective-permute-start.14
  351.1 2.0 fusion.100
  360.7 3.8 collective-permute-done.17
  366.3 3.9 fusion.65
  372.3 2.2 collective-permute-done.19
  379.0 2.0 fusion.99
  384.9 2.1 collective-permute-start.23
  388.6 2.0 collective-permute-done.23
  392.4 6.7 multiply_reduce_fusion.5
  399.1 38.2 %all-reduce.4 = (f32[2]{0:T(128)S(1)}, f32[2]{0:T(128)S(1)}) all-reduce(f32[2]{0:T(128)S(1)} %get-tuple-element.11, f32[2]{0:T(128)S(1)} %get-tuple-element.10), channel_id=1, replica_groups=mesh['gx'=2,'gy'=4,'gz'=4] {'gx','gy','gz'}, use_global_device_ids=true, to_apply=%region_2.0 | all-reduce | flops 4 | bytes 32 | tf_op jit(solution)/shard_map/psum | solution.py:38
  438.8 2.3 collective-permute-start.25
  443.0 2.0 collective-permute-done.24
  448.7 2.0 fusion.98
  458.5 3.8 collective-permute-done.29
  464.1 3.9 fusion.52
  468.2 2.0 collective-permute-start.30
  476.1 2.0 fusion.97
  485.7 2.2 collective-permute-done.35
  489.6 7.1 multiply_reduce_fusion.3
  496.7 38.5 %all-reduce.3 = (f32[2]{0:T(128)S(1)}, f32[2]{0:T(128)S(1)}) all-reduce(f32[2]{0:T(128)S(1)} %get-tuple-element.9, f32[2]{0:T(128)S(1)} %get-tuple-element.8), channel_id=1, replica_groups=mesh['gx'=2,'gy'=4,'gz'=4] {'gx','gy','gz'}, use_global_device_ids=true, to_apply=%region_6.0 | all-reduce | flops 4 | bytes 32 | tf_op jit(solution)/shard_map/psum | solution.py:38
  535.3 2.3 multiply_subtract_fusion.1
  537.6 2.3 collective-permute-start.37
  541.8 2.0 collective-permute-done.36
  547.5 2.0 fusion.96
  557.1 3.8 collective-permute-done.41
  562.6 3.9 fusion.39
  574.8 2.0 fusion.95
  584.4 2.3 collective-permute-done.47
  588.4 7.1 multiply_reduce_fusion.1
  595.5 38.5 %all-reduce.2 = (f32[2]{0:T(128)S(1)}, f32[2]{0:T(128)S(1)}) all-reduce(f32[2]{0:T(128)S(1)} %get-tuple-element.7, f32[2]{0:T(128)S(1)} %get-tuple-element.6), channel_id=1, replica_groups=mesh['gx'=2,'gy'=4,'gz'=4] {'gx','gy','gz'}, use_global_device_ids=true, to_apply=%region_10.0 | all-reduce | flops 4 | bytes 32 | tf_op jit(solution)/shard_map/psum | solution.py:38
  634.0 2.4 multiply_reduce_fusion
  636.4 2.3 collective-permute-start.49
  640.6 2.0 collective-permute-done.48
  646.3 2.0 fusion.94
  656.0 3.8 collective-permute-done.53
  661.5 5.9 fusion.26
  667.5 2.0 collective-permute-start.54
  675.5 2.0 fusion.93
  681.6 2.0 collective-permute-start.59
  685.3 2.4 collective-permute-done.59
  689.5 6.3 fusion.20
  695.8 38.4 %all-reduce.1 = (f32[2]{0:T(128)S(1)}, f32[2]{0:T(128)S(1)}) all-reduce(f32[2]{0:T(128)S(1)} %get-tuple-element.22, f32[2]{0:T(128)S(1)} %fusion.20), channel_id=1, replica_groups=mesh['gx'=2,'gy'=4,'gz'=4] {'gx','gy','gz'}, use_global_device_ids=true, to_apply=%region_14.0 | all-reduce | flops 4 | bytes 32 | tf_op jit(solution)/shard_map/psum | solution.py:38
  734.2 2.7 multiply_add_fusion
  736.9 2.3 collective-permute-start.61
  739.3 2.2 collective-permute-done.61
  741.5 2.0 collective-permute-done.60
  745.4 2.0 collective-permute-done.63
  747.9 3.2 fusion.92
  751.1 2.8 copy.49
  755.5 2.8 copy.51
  759.0 2.6 copy.50
  761.6 3.4 collective-permute-done.65
  765.1 2.6 copy.52
  767.7 6.9 fusion.7
  (233 shorter events, 160.8 us)
Async XLA Ops:
  1.5 7.0 collective-permute-start
  4.5 3.9 collective-permute-start.1
  8.6 3.4 collective-permute-start.3
  8.7 3.4 collective-permute-start.2
  16.3 7.7 collective-permute-start.5
  17.9 4.4 collective-permute-start.4
  30.2 8.1 %collective-permute-start.7 = (f32[2,1,32,128]{3,2,1,0:T(8,128)S(1)}, f32[2,1,32,128]{3,2,1,0:T(8,128)S(1)}, u32[]{:S(2)}, u32[]{:S(2)}) collective-permute-start(f32[2,1,32,128]{3,2,1,0:T(8,128)S(1)} %get-tuple-element.95), channel_id=1, source_target_pairs={{0,16},{16,0},{1,17},{17,1},{2,18},{18,2},{3,19},{19,3},{4,20},{20... | collective-permute-start | bytes 98312 | tf_op jit(solution)/shard_map/ppermute | solution.py:19
  31.2 7.1 collective-permute-start.6
  38.4 154.6 %collective-permute-start.9 = (f32[2,34,1,128]{3,2,1,0:T(1,128)S(1)}, f32[2,34,1,128]{3,2,1,0:T(1,128)S(1)}, u32[]{:S(2)}, u32[]{:S(2)}) collective-permute-start(f32[2,34,1,128]{3,2,1,0:T(1,128)S(1)} %get-tuple-element.75), channel_id=1, source_target_pairs={{0,4},{4,8},{8,12},{12,0},{1,5},{5,9},{9,13},{13,1},{2,6},{6,10},{... | collective-permute-start | bytes 104456 | tf_op jit(solution)/shard_map/ppermute | solution.py:19
  38.4 154.5 %collective-permute-start.8 = (f32[2,34,1,128]{3,2,1,0:T(1,128)S(1)}, f32[2,34,1,128]{3,2,1,0:T(1,128)S(1)}, u32[]{:S(2)}, u32[]{:S(2)}) collective-permute-start(f32[2,34,1,128]{3,2,1,0:T(1,128)S(1)} %get-tuple-element.76), channel_id=1, source_target_pairs={{4,0},{8,4},{12,8},{0,12},{5,1},{9,5},{13,9},{1,13},{6,2},{10,6},{... | collective-permute-start | bytes 104456 | tf_op jit(solution)/shard_map/ppermute | solution.py:20
  197.2 136.8 %collective-permute-start.11 = (f32[2,34,34,1]{2,0,3,1:T(2,128)S(1)}, f32[2,34,34,1]{2,0,3,1:T(2,128)S(1)}, u32[]{:S(2)}, u32[]{:S(2)}) collective-permute-start(f32[2,34,34,1]{2,0,3,1:T(2,128)S(1)} %copy.15), channel_id=1, source_target_pairs={{0,1},{1,2},{2,3},{3,0},{4,5},{5,6},{6,7},{7,4},{8,9},{9,10},{10,1... | collective-permute-start | bytes 27752 | tf_op jit(solution)/shard_map/ppermute | solution.py:19
  199.0 133.2 %collective-permute-start.10 = (f32[2,34,34,1]{2,0,3,1:T(2,128)S(1)}, f32[2,34,34,1]{2,0,3,1:T(2,128)S(1)}, u32[]{:S(2)}, u32[]{:S(2)}) collective-permute-start(f32[2,34,34,1]{2,0,3,1:T(2,128)S(1)} %copy.13), channel_id=1, source_target_pairs={{1,0},{2,1},{3,2},{0,3},{5,4},{6,5},{7,6},{4,7},{9,8},{10,9},{11,1... | collective-permute-start | bytes 27752 | tf_op jit(solution)/shard_map/ppermute | solution.py:20
  342.1 4.0 collective-permute-start.13
  343.1 3.9 collective-permute-start.12
  347.1 3.4 collective-permute-start.15
  347.2 3.7 collective-permute-start.14
  355.0 4.0 collective-permute-start.16
  358.8 5.8 collective-permute-start.17
  370.2 4.3 collective-permute-start.19
  371.4 3.9 collective-permute-start.18
  375.4 3.4 collective-permute-start.21
  382.9 4.0 collective-permute-start.22
  384.9 5.8 collective-permute-start.23
  438.8 4.2 collective-permute-start.25
  441.1 3.9 collective-permute-start.24
  445.1 3.4 collective-permute-start.27
  445.2 3.4 collective-permute-start.26
  452.6 4.2 collective-permute-start.28
  456.1 6.2 collective-permute-start.29
  468.0 4.0 collective-permute-start.31
  468.2 4.2 collective-permute-start.30
  472.4 3.4 collective-permute-start.33
  472.5 3.4 collective-permute-start.32
  480.0 4.0 collective-permute-start.34
  482.1 5.8 collective-permute-start.35
  537.6 4.2 collective-permute-start.37
  539.9 3.9 collective-permute-start.36
  543.9 3.4 collective-permute-start.39
  543.9 3.4 collective-permute-start.38
  551.4 4.0 collective-permute-start.40
  554.9 6.0 collective-permute-start.41
  566.5 4.0 collective-permute-start.43
  566.8 4.1 collective-permute-start.42
  570.9 3.4 collective-permute-start.45
  571.0 3.5 collective-permute-start.44
  578.6 4.0 collective-permute-start.46
  580.9 5.8 collective-permute-start.47
  636.4 4.2 collective-permute-start.49
  638.7 3.9 collective-permute-start.48
  642.7 3.4 collective-permute-start.51
  642.7 3.4 collective-permute-start.50
  650.2 4.1 collective-permute-start.52
  653.7 6.1 collective-permute-start.53
  667.4 4.0 collective-permute-start.55
  667.5 4.2 collective-permute-start.54
  671.8 3.4 collective-permute-start.57
  679.3 4.3 collective-permute-start.58
  681.6 6.2 collective-permute-start.59
  736.9 4.6 collective-permute-start.61
  739.3 4.3 collective-permute-start.60
  743.6 3.8 collective-permute-start.63
  743.7 3.7 collective-permute-start.62
  753.9 5.1 collective-permute-start.64
  758.3 6.7 collective-permute-start.65
  (20 other events, 386.4 us)
where the time goes:
time: 784 us; the launch traced here: 776 us
  local copies, waits for them, and re-layouts  238 us (30%)
  other arithmetic  235 us (30%)
  blocking collectives  154 us (20%)
  waiting for transfers between devices  75.2 us (10%)
  starting transfers between devices  73 us (9%)
    unnamed x6, other arithmetic  156 us
    psum x4, blocking collectives, two_products(): lax.psum((jnp.sum(residual * residual, axis=(1, 2, 3)), jnp.sum(residual...  154 us
    slice x1, local copies, waits for them, and re-layouts, on_device(): counted = scattered[0].reshape(field_shape)  131 us
    ppermute x33, waiting for transfers between devices, with_halo(): before = lax.ppermute(last, axis, up)  61.8 us
    ppermute x33, starting transfers between devices, with_halo(): after = lax.ppermute(leading, axis, down)  45.6 us
    slice x23, local copies, waits for them, and re-layouts, with_halo(): leading = lax.slice_in_dim(shard, 0, width, axis=dim)  44.8 us
    sub x6, other arithmetic, stencil(): return (kappa_sq[None] + 6.0) * center - beside  29.1 us
    ppermute x33, starting transfers between devices, with_halo(): before = lax.ppermute(last, axis, up)  27.5 us
  transfers between devices with their start and end apart: 66, of which 41 were waited for; matrix products, arithmetic and copies ran while one was open for 43% of the time, Pallas kernels for 0%

commit v1 on v0

v1 whole, which is shorter than its diff:
```python
import functools
import itertools

import jax
import jax.numpy as jnp
from jax import lax
from jax.experimental import pallas as pl
from jax.experimental.pallas import tpu as pltpu
from jax.sharding import PartitionSpec as P

ITERS = 4
LANES = 128
AXES = ("gx", "gy", "gz")
MESH = pl.DeviceIdType.MESH

noise_var = 0.25


def kernel(
    sizes, dims, lr_ref, state_ref, start_ref, idx_ref, val_ref, grad_ref, adj_ref,
    ext, ysend, yrecv, zsend, zrecv, kap, weight, values, rhs_hot, res, image,
    xi, ast, res_image, d, di, s_buf, z_buf, q_buf, red_out, red, send_sem, recv_sem, red_send, red_recv,
):
    sets, cx, cy, cz, nobs = dims
    rows = cx * cy
    place = [lax.axis_index(axis) for axis in AXES]
    rank = (place[0] * sizes[1] + place[1]) * sizes[2] + place[2]
    total = sizes[0] * sizes[1] * sizes[2]
    lane = lax.broadcasted_iota(jnp.int32, (cy, LANES), 1)
    row = lax.broadcasted_iota(jnp.int32, (cy, LANES), 0)
    small_lane = lax.broadcasted_iota(jnp.int32, (1, LANES), 1)
    offsets = [o for o in itertools.product(*[range(n) for n in sizes]) if any(o)]

    def device_at(offset):
        return tuple(lax.rem(p + o, n) for p, o, n in zip(place, offset, sizes))

    barrier = pltpu.get_barrier_semaphore()
    for offset in offsets:
        pl.semaphore_signal(barrier, inc=1, device_id=device_at(offset), device_id_type=MESH)

    def inner(x):
        return pl.ds(pl.multiple_of((x + 1) * cy, cy), cy)

    def plain(x):
        return pl.ds(pl.multiple_of(x * cy, cy), cy)

    def fold(v):
        return jnp.sum(v.reshape(cy // 8, 8, LANES), axis=0)

    def sweep(body, slot=None, sums=0):
        zero = jnp.zeros((cy, LANES), jnp.float32)
        faces = (zero, zero) if slot is not None else ()
        gathered = []
        for s in range(sets):
            def step(x, carry, s=s):
                faces, acc = carry
                slab, terms = body(s, x)
                if slot is not None:
                    at = s * cx + x
                    here = lane == at
                    low = jnp.where(here, pltpu.roll(slab, at, 1), faces[0])
                    high = jnp.where(here, pltpu.roll(slab, at + 1, 1), faces[1])
                    faces = (low, high)
                acc = tuple(a + fold(t) for a, t in zip(acc, terms))
                return faces, acc
            acc = tuple(jnp.zeros((8, LANES), jnp.float32) for _ in range(sums))
            faces, acc = lax.fori_loop(0, cx, step, (faces, acc), unroll=4)
            gathered.append(acc)
        if slot is not None:
            zsend[slot, 0] = faces[0]
            zsend[slot, 1] = faces[1]
            for s in range(sets):
                ysend[slot, 0, s * cx:(s + 1) * cx] = ext[slot, s, pl.ds(cy, cx, stride=cy), :]
                ysend[slot, 1, s * cx:(s + 1) * cx] = ext[slot, s, pl.ds(2 * cy - 1, cx, stride=cy), :]
        return gathered

    def copies(slot):
        near = [[tuple(sign if i == axis else 0 for i in range(3)) for sign in (-1, 1)] for axis in range(3)]
        ends = [
            (ext.at[slot, :, pl.ds(cy, cy), :], ext.at[slot, :, pl.ds((cx + 1) * cy, cy), :]),
            (ext.at[slot, :, pl.ds(cx * cy, cy), :], ext.at[slot, :, pl.ds(0, cy), :]),
            (ysend.at[slot, 0], yrecv.at[slot, 1]),
            (ysend.at[slot, 1], yrecv.at[slot, 0]),
            (zsend.at[slot, 0], zrecv.at[slot, 1]),
            (zsend.at[slot, 1], zrecv.at[slot, 0]),
        ]
        out = []
        for n, (src, dst) in enumerate(ends):
            offset = tuple(o % size for o, size in zip(near[n // 2][n % 2], sizes))
            out.append(pltpu.make_async_remote_copy(
                src_ref=src, dst_ref=dst, send_sem=send_sem.at[slot, n], recv_sem=recv_sem.at[slot, n],
                device_id=device_at(offset), device_id_type=MESH))
        return out

    def send(slot):
        for copy in copies(slot):
            copy.start()

    def arrive(slot):
        for copy in copies(slot):
            copy.wait()

    def apply(slot, s, x):
        center = ext[slot, s, inner(x), :]
        beside = ext[slot, s, inner(x + 1), :] + ext[slot, s, inner(x - 1), :]
        before = yrecv[slot, 0, pl.ds(s * cx + x, 1), :]
        after = yrecv[slot, 1, pl.ds(s * cx + x, 1), :]
        beside = beside + jnp.where(row == cy - 1, after, pltpu.roll(center, cy - 1, 0))
        beside = beside + jnp.where(row == 0, before, pltpu.roll(center, 1, 0))
        turn = LANES - 1 - (s * cx + x)
        low = pltpu.roll(zrecv[slot, 0], turn, 1)
        high = pltpu.roll(zrecv[slot, 1], turn + 1, 1)
        beside = beside + pltpu.roll(jnp.where(lane == 0, high, center), LANES - 1, 1)
        beside = beside + pltpu.roll(jnp.where(lane == LANES - 1, low, center), 1, 1)
        return (kap[plain(x), :] + 6.0) * center - beside

    def reduce_start(n, gathered):
        line = jnp.zeros((1, LANES), jnp.float32)
        for s in range(sets):
            for j in range(2):
                value = jnp.sum(jnp.sum(gathered[s][j], axis=0, keepdims=True), axis=1, keepdims=True)
                line = jnp.where(small_lane == 2 * s + j, value, line)
        red_out[n] = line
        red[n, rank] = line
        for offset in offsets:
            pltpu.make_async_remote_copy(
                src_ref=red_out.at[n], dst_ref=red.at[n, rank], send_sem=red_send.at[n],
                recv_sem=red_recv.at[n], device_id=device_at(offset), device_id_type=MESH).start()

    def reduce_end(n):
        many = red.at[n, pl.ds(0, total - 1)]
        pltpu.make_async_copy(many, many, red_recv.at[n]).wait()
        pltpu.make_async_copy(many, many, red_send.at[n]).wait()
        line = jnp.sum(red[n], axis=0)
        def pick(j):
            value = jnp.sum(jnp.where(small_lane == j, line, 0.0), axis=1, keepdims=True)
            return jnp.broadcast_to(value, (1, LANES))
        return [(pick(2 * s), pick(2 * s + 1)) for s in range(sets)]

    def load(slot, ref):
        def body(s, x):
            slab = ref[s, plain(x), :]
            ext[slot, s, inner(x), :] = slab
            return slab, ()
        sweep(body, slot)

    load(0, start_ref)
    load(2, state_ref)
    pl.semaphore_wait(barrier, total - 1)
    send(0)
    send(2)

    kap[...] = 4.0 * jnp.exp(-2.0 * lr_ref[...])

    tile = min(rows, 256)
    hot_lane = lax.broadcasted_iota(jnp.int32, (LANES, nobs), 0)
    for s in range(sets):
        cell = idx_ref[s:s + 1, :]
        value = val_ref[s:s + 1, :]
        hit = hot_lane == cell % cz
        top = value.astype(jnp.bfloat16).astype(jnp.float32)
        rhs_hot[0:LANES] = jnp.where(hit, 1.0, 0.0).astype(jnp.bfloat16)
        rhs_hot[LANES:2 * LANES] = jnp.where(hit, top, 0.0).astype(jnp.bfloat16)
        rhs_hot[2 * LANES:] = jnp.where(hit, value - top, 0.0).astype(jnp.bfloat16)
        line = cell // cz

        def step(m, carry, s=s, line=line):
            base = m * tile
            ids = lax.broadcasted_iota(jnp.int32, (tile, nobs), 0) + base
            hot = jnp.where(ids == line, 1.0, 0.0).astype(jnp.bfloat16)
            got = lax.dot_general(hot, rhs_hot[...], (((1,), (1,)), ((), ())), preferred_element_type=jnp.float32)
            at = pl.ds(pl.multiple_of(base, tile), tile)
            weight[s, at, :] = got[:, :LANES] * (1.0 / noise_var)
            values[s, at, :] = (got[:, LANES:2 * LANES] + got[:, 2 * LANES:]) * (1.0 / noise_var)
            return carry
        lax.fori_loop(0, rows // tile, step, 0)

    def start_pass(s, x):
        out = apply(0, s, x)
        ext[1, s, inner(x), :] = out
        xi[s, plain(x), :] = out
        return out, ()

    arrive(0)
    sweep(start_pass, 1)
    send(1)

    def right_pass(s, x):
        at = plain(x)
        right = values[s, at, :] - weight[s, at, :] * (state_ref[s, at, :] + start_ref[s, at, :])
        res[s, at, :] = right
        return right, ()

    sweep(right_pass)
    arrive(1)

    def residual_pass(s, x):
        out = res[s, plain(x), :] - apply(1, s, x)
        res[s, plain(x), :] = out
        ext[0, s, inner(x), :] = out
        return out, ()

    sweep(residual_pass, 0)
    send(0)

    def state_pass(s, x):
        out = apply(2, s, x)
        ast[s, plain(x), :] = out
        return out, ()

    arrive(2)
    sweep(state_pass)
    arrive(0)

    def inner_pass(s, x):
        out = apply(0, s, x)
        ext[1, s, inner(x), :] = out
        res_image[s, plain(x), :] = out
        return out, ()

    sweep(inner_pass, 1)
    send(1)
    arrive(1)

    def image_pass(s, x):
        now = res[s, plain(x), :]
        out = apply(1, s, x) + weight[s, plain(x), :] * now
        ext[0, s, inner(x), :] = out
        return out, (now * now, now * out)

    gathered = sweep(image_pass, 0, 2)
    send(0)
    reduce_start(0, gathered)

    def next_inner(s, x):
        out = apply(0, s, x)
        ext[1, s, inner(x), :] = out
        return out, ()

    def next_image(s, x):
        out = apply(1, s, x) + weight[s, plain(x), :] * ext[0, s, inner(x), :]
        image[s, plain(x), :] = out
        return out, ()

    norms = steps = None
    for k in range(ITERS):
        last = k + 1 == ITERS
        if not last:
            arrive(0)
            sweep(next_inner, 1)
            send(1)
            arrive(1)
            sweep(next_image)
        sums = reduce_end(k)
        if k == 0:
            ratio = None
            step_size = [norm / product for norm, product in sums]
        else:
            ratio = [sums[s][0] / norms[s] for s in range(sets)]
            step_size = [sums[s][0] / (sums[s][1] - ratio[s] * sums[s][0] / steps[s]) for s in range(sets)]
        norms, steps = [norm for norm, product in sums], step_size

        def follow(buf, s, at, new, ratio=ratio):
            if ratio is not None:
                new = new + ratio[s] * buf[s, at, :]
            return new

        if last:
            def finish(x, carry):
                at = plain(x)
                grad = jnp.zeros((cy, LANES), jnp.float32)
                for s in range(sets):
                    adj = adj_ref[s, at, :] + step_size[s] * follow(d, s, at, res[s, at, :])
                    adj_ref[s, at, :] = adj
                    applied = xi[s, at, :] + step_size[s] * follow(di, s, at, res_image[s, at, :])
                    grad = grad + (adj * ast[s, at, :] + applied * state_ref[s, at, :])
                grad_ref[at, :] = -2.0 * kap[at, :] * grad
                return carry
            lax.fori_loop(0, cx, finish, 0, unroll=2)
            break

        def update(s, x):
            at = plain(x)
            now, vec = res[s, at, :], ext[0, s, inner(x), :]
            z_new = follow(z_buf, s, at, image[s, at, :])
            s_new = follow(s_buf, s, at, vec)
            d[s, at, :] = follow(d, s, at, now)
            z_buf[s, at, :] = z_new
            s_buf[s, at, :] = s_new
            vec = vec - step_size[s] * z_new
            now = now - step_size[s] * s_new
            ext[0, s, inner(x), :] = vec
            res[s, at, :] = now
            return vec, (now * now, now * vec)

        more = k + 2 < ITERS
        gathered = sweep(update, 0 if more else None, 2)
        if more:
            send(0)
        reduce_start(k + 1, gathered)

        def trail(s, x):
            at = plain(x)
            base = start_ref if k == 0 else adj_ref
            adj_ref[s, at, :] = base[s, at, :] + step_size[s] * d[s, at, :]
            di_new = follow(di, s, at, res_image[s, at, :])
            di[s, at, :] = di_new
            xi[s, at, :] = xi[s, at, :] + step_size[s] * di_new
            q_new = follow(q_buf, s, at, ext[1, s, inner(x), :])
            q_buf[s, at, :] = q_new
            res_image[s, at, :] = res_image[s, at, :] - step_size[s] * q_new
            return q_new, ()

        sweep(trail)


def on_device(sizes, log_range, state, adjoint_start, obs_index, obs_value):
    sets, cx, cy, cz = state.shape
    nobs = obs_index.shape[-1]
    rows = cx * cy
    total = sizes[0] * sizes[1] * sizes[2]
    field = pltpu.VMEM((sets, rows, cz), jnp.float32)
    vmem = pl.BlockSpec(memory_space=pltpu.VMEM)
    gradient, adjoint = pl.pallas_call(
        functools.partial(kernel, sizes, (sets, cx, cy, cz, nobs)),
        out_shape=(
            jax.ShapeDtypeStruct((rows, cz), jnp.float32),
            jax.ShapeDtypeStruct((sets, rows, cz), jnp.float32),
        ),
        in_specs=[vmem] * 5,
        out_specs=(vmem, vmem),
        scratch_shapes=[
            pltpu.VMEM((3, sets, rows + 2 * cy, cz), jnp.float32),
            pltpu.VMEM((3, 2, sets * cx, cz), jnp.float32),
            pltpu.VMEM((3, 2, sets * cx, cz), jnp.float32),
            pltpu.VMEM((3, 2, cy, LANES), jnp.float32),
            pltpu.VMEM((3, 2, cy, LANES), jnp.float32),
            pltpu.VMEM((rows, cz), jnp.float32),
            field,
            field,
            pltpu.VMEM((3 * LANES, nobs), jnp.bfloat16),
            *([field] * 10),
            pltpu.VMEM((ITERS, 1, LANES), jnp.float32),
            pltpu.VMEM((ITERS, total, 1, LANES), jnp.float32),
            pltpu.SemaphoreType.DMA((3, 6)),
            pltpu.SemaphoreType.DMA((3, 6)),
            pltpu.SemaphoreType.DMA((ITERS,)),
            pltpu.SemaphoreType.DMA((ITERS,)),
        ],
        compiler_params=pltpu.CompilerParams(
            collective_id=0, has_side_effects=True, vmem_limit_bytes=60 * 1024 * 1024
        ),
    )(
        log_range.reshape(rows, cz),
        state.reshape(sets, rows, cz),
        adjoint_start.reshape(sets, rows, cz),
        obs_index.reshape(sets, nobs),
        obs_value.reshape(sets, nobs),
    )
    return gradient.reshape(cx, cy, cz), adjoint.reshape(sets, cx, cy, cz)


def solution(mesh):
    in_specs = (
        P("gx", "gy", "gz"),
        P(None, "gx", "gy", "gz"),
        P(None, "gx", "gy", "gz"),
        P(None, "gx", "gy", "gz", None),
        P(None, "gx", "gy", "gz", None),
    )
    out_specs = (P("gx", "gy", "gz"), P(None, "gx", "gy", "gz"))
    sizes = tuple(mesh.shape[axis] for axis in AXES)
    return jax.shard_map(
        functools.partial(on_device, sizes), mesh=mesh, in_specs=in_specs, out_specs=out_specs, check_vma=False
    )
```

time: 784 us -> 109 us (0.14)
  other arithmetic: 235 us -> 0 us
  local copies, waits for them, and re-layouts: 238 us -> 4.98 us
  blocking collectives: 154 us -> 0 us
  Pallas kernels: 0 us -> 103 us
  waiting for transfers between devices: 75.2 us -> 0 us
  starting transfers between devices: 73 us -> 0 us
    slice x45 -> x0, local copies, waits for them, and re-layouts: 195 us -> none  [the longest x1 131 us: on_device(): counted = scattered[0].reshape(field_shape)]
    unnamed x6 -> x0, other arithmetic: 156 us -> none
    psum x4 -> x0, blocking collectives: 154 us -> none  [two_products(): lax.psum((jnp.sum(residual * residual, axis=(1, 2, 3)), jnp.sum(residual...]
    pallas_call x0 -> x1, Pallas kernels: none -> 103 us  [on_device(): pl.pallas_call(functools.partial(kernel, sizes, (sets, cx, cy, cz, nobs))...]
    ppermute x66 -> x0, waiting for transfers between devices: 75.2 us -> none  [the longest x33 61.8 us: with_halo(): before = lax.ppermute(last, axis, up)]
    ppermute x66 -> x0, starting transfers between devices: 73 us -> none  [the longest x33 45.6 us: with_halo(): after = lax.ppermute(leading, axis, down)]
    ppermute x22 -> x0, local copies, waits for them, and re-layouts: 39.4 us -> none  [the longest x11 19.7 us: with_halo(): before = lax.ppermute(last, axis, up)]
    sub x9 -> x0, other arithmetic: 39.2 us -> none  [the longest x6 29.1 us: stencil(): return (kappa_sq[None] + 6.0) * center - beside]
  transfers between devices with their start and end apart: 66 -> 0, of which waited for: 41 -> 0; matrix products, arithmetic and copies ran while one was open for 43% -> 0% of each run, Pallas kernels for 0% -> 0%
where the time goes in v1:
time: 109 us; the launch traced here: 108 us
  Pallas kernels  103 us (94%)
  local copies, waits for them, and re-layouts  4.98 us (5%)
    pallas_call x1, Pallas kernels, on_device(): pl.pallas_call(functools.partial(kernel, sizes, (sets, cx, cy, cz, nobs))...  103 us
    unnamed x8, local copies, waits for them, and re-layouts  4.98 us

profile of v1, /device:TPU:0, one launch (start us, length us, event | category | flops | bytes accessed | tf_op | source)
XLA Modules:
  0.0 108.4 jit_solution(1543088846021396315)
XLA Ops:
  0.6 0.0 copy-start.1
  0.6 1.4 %copy.12 = s32[2,1,1,1,4096]{4,0,2,1,3:T(2,128)} copy(s32[2,1,1,1,4096]{4,3,2,1,0:T(1,128)} %param.8) | data formatting | bytes 65536
  2.0 0.0 copy-done.1
  2.0 0.6 copy.11
  2.7 102.8 %shard_map.68 = (f32[1024,128]{1,0:T(8,128)}, f32[2,1024,128]{2,1,0:T(8,128)}) custom-call(f32[1024,128]{1,0:T(8,128)} %bitcast.15, f32[2,1024,128]{2,1,0:T(8,128)} %bitcast.12, f32[2,1024,128]{2,1,0:T(8,128)} %bitcast.13, s32[2,4096]{1,0:T(2,128)} %bitcast.16, f32[2,4096]{1,0:T(2,128)} %bitcast.17), custom_call_target="tpu_custom_call" | custom-call | tf_op jit(solution)/shard_map/pallas_call | solution.py:324
  105.5 0.0 copy-start
  105.5 2.0 %copy.15 = f32[32,32,128]{2,1,0:T(8,128)} copy(f32[32,32,128]{2,1,0:T(8,128)} %bitcast.14) | data formatting | bytes 1048576
  107.4 0.0 copy-done
  107.4 1.0 copy.16
Async XLA Ops:
  0.6 1.4 %copy-start.1 = (f32[2,1,1,1,4096]{4,3,2,1,0:T(1,128)S(1)}, f32[2,1,1,1,4096]{4,3,2,1,0:T(1,128)}, u32[]{:S(2)}) copy-start(f32[2,1,1,1,4096]{4,3,2,1,0:T(1,128)} %param.9) | copy-start | bytes 98308
  105.5 2.0 %copy-start = (f32[2,1024,128]{2,1,0:T(8,128)S(1)}, f32[2,1024,128]{2,1,0:T(8,128)}, u32[]{:S(2)}) copy-start(f32[2,1024,128]{2,1,0:T(8,128)} %get-tuple-element.5) | copy-start | bytes 3145732

commit v2 on v1

--- a/solution.py
+++ b/solution.py
@@ -18,7 +18,7 @@
 
 def kernel(
     sizes, dims, lr_ref, state_ref, start_ref, idx_ref, val_ref, grad_ref, adj_ref,
-    ext, ysend, yrecv, zsend, zrecv, kap, weight, values, rhs_hot, res, image,
+    ext, ysend, yrecv, zsend, zrecv, zboth, kap, weight, values, rhs_hot, res, image,
     xi, ast, res_image, d, di, s_buf, z_buf, q_buf, red_out, red, send_sem, recv_sem, red_send, red_recv,
 ):
     sets, cx, cy, cz, nobs = dims
@@ -28,6 +28,8 @@
     total = sizes[0] * sizes[1] * sizes[2]
     lane = lax.broadcasted_iota(jnp.int32, (cy, LANES), 1)
     row = lax.broadcasted_iota(jnp.int32, (cy, LANES), 0)
+    pair = lane // 2
+    even = lane % 2 == 0
     small_lane = lax.broadcasted_iota(jnp.int32, (1, LANES), 1)
     offsets = [o for o in itertools.product(*[range(n) for n in sizes]) if any(o)]
 
@@ -49,26 +51,23 @@
 
     def sweep(body, slot=None, sums=0):
         zero = jnp.zeros((cy, LANES), jnp.float32)
-        faces = (zero, zero) if slot is not None else ()
-        gathered = []
-        for s in range(sets):
-            def step(x, carry, s=s):
-                faces, acc = carry
+        faces = (zero,) * sets if slot is not None else ()
+
+        def step(x, carry):
+            faces, gathered = carry
+            packed, added = [], []
+            for s in range(sets):
                 slab, terms = body(s, x)
                 if slot is not None:
                     at = s * cx + x
-                    here = lane == at
-                    low = jnp.where(here, pltpu.roll(slab, at, 1), faces[0])
-                    high = jnp.where(here, pltpu.roll(slab, at + 1, 1), faces[1])
-                    faces = (low, high)
-                acc = tuple(a + fold(t) for a, t in zip(acc, terms))
-                return faces, acc
-            acc = tuple(jnp.zeros((8, LANES), jnp.float32) for _ in range(sums))
-            faces, acc = lax.fori_loop(0, cx, step, (faces, acc), unroll=4)
-            gathered.append(acc)
+                    packed.append(jnp.where(pair == at, pltpu.roll(slab, 2 * at + 1, 1), faces[s]))
+                added.append(tuple(a + fold(t) for a, t in zip(gathered[s], terms)))
+            return tuple(packed), tuple(added)
+
+        start = tuple(tuple(jnp.zeros((8, LANES), jnp.float32) for _ in range(sums)) for _ in range(sets))
+        faces, gathered = lax.fori_loop(0, cx, step, (faces, start), unroll=8)
         if slot is not None:
-            zsend[slot, 0] = faces[0]
-            zsend[slot, 1] = faces[1]
+            zsend[slot] = functools.reduce(jnp.add, faces)
             for s in range(sets):
                 ysend[slot, 0, s * cx:(s + 1) * cx] = ext[slot, s, pl.ds(cy, cx, stride=cy), :]
                 ysend[slot, 1, s * cx:(s + 1) * cx] = ext[slot, s, pl.ds(2 * cy - 1, cx, stride=cy), :]
@@ -81,8 +80,8 @@
             (ext.at[slot, :, pl.ds(cx * cy, cy), :], ext.at[slot, :, pl.ds(0, cy), :]),
             (ysend.at[slot, 0], yrecv.at[slot, 1]),
             (ysend.at[slot, 1], yrecv.at[slot, 0]),
-            (zsend.at[slot, 0], zrecv.at[slot, 1]),
-            (zsend.at[slot, 1], zrecv.at[slot, 0]),
+            (zsend.at[slot], zrecv.at[slot, 1]),
+            (zsend.at[slot], zrecv.at[slot, 0]),
         ]
         out = []
         for n, (src, dst) in enumerate(ends):
@@ -99,19 +98,19 @@
     def arrive(slot):
         for copy in copies(slot):
             copy.wait()
+        zboth[slot] = jnp.where(even, zrecv[slot, 0], pltpu.roll(zrecv[slot, 1], LANES - 2, 1))
 
     def apply(slot, s, x):
         center = ext[slot, s, inner(x), :]
         beside = ext[slot, s, inner(x + 1), :] + ext[slot, s, inner(x - 1), :]
         before = yrecv[slot, 0, pl.ds(s * cx + x, 1), :]
         after = yrecv[slot, 1, pl.ds(s * cx + x, 1), :]
+        base = (x + 1) * cy
         beside = beside + jnp.where(row == cy - 1, after, pltpu.roll(center, cy - 1, 0))
         beside = beside + jnp.where(row == 0, before, pltpu.roll(center, 1, 0))
-        turn = LANES - 1 - (s * cx + x)
-        low = pltpu.roll(zrecv[slot, 0], turn, 1)
-        high = pltpu.roll(zrecv[slot, 1], turn + 1, 1)
-        beside = beside + pltpu.roll(jnp.where(lane == 0, high, center), LANES - 1, 1)
-        beside = beside + pltpu.roll(jnp.where(lane == LANES - 1, low, center), 1, 1)
+        edge = pltpu.roll(zboth[slot], lax.rem(LANES - 2 * (s * cx + x), LANES), 1)
+        beside = beside + jnp.where(lane == LANES - 1, edge, pltpu.roll(center, LANES - 1, 1))
+        beside = beside + jnp.where(lane == 0, edge, pltpu.roll(center, 1, 1))
         return (kap[plain(x), :] + 6.0) * center - beside
 
     def reduce_start(n, gathered):
@@ -276,7 +275,7 @@
                     grad = grad + (adj * ast[s, at, :] + applied * state_ref[s, at, :])
                 grad_ref[at, :] = -2.0 * kap[at, :] * grad
                 return carry
-            lax.fori_loop(0, cx, finish, 0, unroll=2)
+            lax.fori_loop(0, cx, finish, 0, unroll=8)
             break
 
         def update(s, x):
@@ -333,8 +332,9 @@
             pltpu.VMEM((3, sets, rows + 2 * cy, cz), jnp.float32),
             pltpu.VMEM((3, 2, sets * cx, cz), jnp.float32),
             pltpu.VMEM((3, 2, sets * cx, cz), jnp.float32),
+            pltpu.VMEM((3, cy, LANES), jnp.float32),
             pltpu.VMEM((3, 2, cy, LANES), jnp.float32),
-            pltpu.VMEM((3, 2, cy, LANES), jnp.float32),
+            pltpu.VMEM((3, cy, LANES), jnp.float32),
             pltpu.VMEM((rows, cz), jnp.float32),
             field,
             field,

time: 109 us -> 96 us (0.88)
  Pallas kernels: 103 us -> 90.1 us
    pallas_call x1, Pallas kernels: 103 us -> 90.1 us  [on_device(): pl.pallas_call(functools.partial(kernel, sizes, (sets, cx, cy, cz, nobs))...]
where the time goes in v2:
time: 96 us; the launch traced here: 95.8 us
  Pallas kernels  90.1 us (94%)
  local copies, waits for them, and re-layouts  4.98 us (5%)
    pallas_call x1, Pallas kernels, on_device(): pl.pallas_call(functools.partial(kernel, sizes, (sets, cx, cy, cz, nobs))...  90.1 us
    unnamed x8, local copies, waits for them, and re-layouts  4.98 us

profile of v2, /device:TPU:0, one launch (start us, length us, event | category | flops | bytes accessed | tf_op | source)
XLA Modules:
  0.0 95.8 jit_solution(10787843115729625813)
XLA Ops:
  0.6 0.0 copy-start.1
  0.6 1.4 %copy.12 = s32[2,1,1,1,4096]{4,0,2,1,3:T(2,128)} copy(s32[2,1,1,1,4096]{4,3,2,1,0:T(1,128)} %param.8) | data formatting | bytes 65536
  2.0 0.0 copy-done.1
  2.0 0.6 copy.11
  2.7 90.1 %shard_map.68 = (f32[1024,128]{1,0:T(8,128)}, f32[2,1024,128]{2,1,0:T(8,128)}) custom-call(f32[1024,128]{1,0:T(8,128)} %bitcast.15, f32[2,1024,128]{2,1,0:T(8,128)} %bitcast.12, f32[2,1024,128]{2,1,0:T(8,128)} %bitcast.13, s32[2,4096]{1,0:T(2,128)} %bitcast.16, f32[2,4096]{1,0:T(2,128)} %bitcast.17), custom_call_target="tpu_custom_call" | custom-call | tf_op jit(solution)/shard_map/pallas_call | solution.py:323
  92.8 0.0 copy-start
  92.8 2.0 %copy.15 = f32[32,32,128]{2,1,0:T(8,128)} copy(f32[32,32,128]{2,1,0:T(8,128)} %bitcast.14) | data formatting | bytes 1048576
  94.8 0.0 copy-done
  94.8 1.0 %copy.16 = f32[2,32,32,128]{3,2,1,0:T(8,128)} copy(f32[2,32,32,128]{3,2,1,0:T(8,128)S(1)} %bitcast.11) | data formatting | bytes 2097152
Async XLA Ops:
  0.6 1.4 %copy-start.1 = (f32[2,1,1,1,4096]{4,3,2,1,0:T(1,128)S(1)}, f32[2,1,1,1,4096]{4,3,2,1,0:T(1,128)}, u32[]{:S(2)}) copy-start(f32[2,1,1,1,4096]{4,3,2,1,0:T(1,128)} %param.9) | copy-start | bytes 98308
  92.8 2.0 %copy-start = (f32[2,1024,128]{2,1,0:T(8,128)S(1)}, f32[2,1024,128]{2,1,0:T(8,128)}, u32[]{:S(2)}) copy-start(f32[2,1024,128]{2,1,0:T(8,128)} %get-tuple-element.5) | copy-start | bytes 3145732
